TPU v7x, 256 devices: a whole 4x4x8 slice. The times are simulated.
256 devices in a mesh: row: 32 (over y, x, core), col: 8 (over z).
Axes of the slice: x: 4, y: 4, z: 8, core: 2. Of those that a mesh axis runs over, the one named last changes fastest.
Arguments:
- vectors_window: float32 [32, 32, 64, 1024], P(None, 'row', None, 'col'), may hold values from -6 to 6
- column_strip: float32 [32, 32, 64, 1024], P(None, 'row', None, 'col'), may hold values from -6 to 6
- row_strip: float32 [1024, 64, 8, 128], P('row', None, 'col'), may hold values from -6 to 6
- factor: float32 [1024, 1024], P('row', 'col'), may hold values from -2 to 2
- window_start: int32 [1], replicated, may hold values from 1 to 64512
- deflated: int32 [1], replicated, may hold values from 0 to 512
Outputs:
- vectors_updated: float32 [32, 32, 64, 1024], P(None, 'row', None, 'col')
- column_updated: float32 [32, 32, 64, 1024], P(None, 'row', None, 'col')
- row_updated: float32 [1024, 64, 8, 128], P('row', None, 'col')
All inputs are finite; a program needn't handle non-finite values.
Results may differ from a plain program's by a relative error of at most 0.0003.
Values sent between devices are 32-bit elements; how exact they have to be, the bound alone decides.
A program may use at most 64 MiB of HBM per device.

v0:
```python
import jax
import jax.numpy as jnp
from jax import lax
from jax.sharding import PartitionSpec as P

W = 1024


def from_everyone(x, axis):
    peers = lax.axis_size(axis)
    return lax.all_to_all(jnp.broadcast_to(x[None], (peers, *x.shape)), axis, 0, 0, tiled=True)


def laid_out(pieces, dim):
    dims = list(pieces.shape[1:])
    dims[dim] *= pieces.shape[0]
    return jnp.moveaxis(pieces, 0, dim).reshape(dims)


def gather_directly(x, axis, dim):
    pieces = from_everyone(x, axis)
    return laid_out(pieces, dim)


def reflect(factor, deflated):
    columns = jnp.arange(W, dtype=jnp.int32)
    kept_count = W - deflated[0]
    spike_row = jnp.where(columns < kept_count, factor[0], 0.0)
    squares = jnp.sum(spike_row * spike_row)
    corner = factor[0, 0]
    magnitude = jnp.sqrt(squares + 1e-06)
    signum = jnp.where(corner >= 0, 1.0, -1.0)
    vector = spike_row + jnp.where(columns == 0, signum * magnitude, 0.0)
    denominator = squares + 2.0 * jnp.abs(corner) * magnitude + magnitude * magnitude
    scaling = 2.0 / denominator
    reflected_image = jnp.dot(factor, vector, precision=lax.Precision.HIGHEST)
    return factor - scaling * reflected_image[:, None] * vector[None, :]


def body(vectors_window, column_strip, row_strip, factor, window_start, deflated):
    highest = lax.Precision.HIGHEST
    row_position = lax.axis_index("row")
    column_position = lax.axis_index("col")
    start_row = window_start[0]
    widened = gather_directly(factor, "col", 1)
    rotation = reflect(lax.all_gather(widened, "row", axis=0, tiled=True), deflated)
    rounds = vectors_window.shape[0]
    blocks = vectors_window.shape[2]
    local_width = vectors_window.shape[3]
    z_blocks = vectors_window.reshape(rounds, blocks, local_width)
    strip_blocks = column_strip.reshape(rounds, blocks, local_width)
    z_turned = jnp.einsum(
        "rbk,kj->rbj",
        lax.all_to_all(z_blocks, "col", split_axis=1, concat_axis=2, tiled=True),
        rotation,
        precision=highest,
    )
    strip_turned = jnp.einsum(
        "rbk,kj->rbj",
        lax.all_to_all(strip_blocks, "col", split_axis=1, concat_axis=2, tiled=True),
        rotation,
        precision=highest,
    )
    z_rotated = lax.all_to_all(z_turned, "col", split_axis=2, concat_axis=1, tiled=True)
    strip_rotated = lax.all_to_all(strip_turned, "col", split_axis=2, concat_axis=1, tiled=True)
    row_count = lax.axis_size("row")
    round_number = jnp.arange(rounds, dtype=jnp.int32)[:, None]
    block_number = jnp.arange(blocks, dtype=jnp.int32)[None, :]
    row_number = (round_number * row_count + row_position) * blocks + block_number
    column_updated = jnp.where(
        row_number[:, :, None] < start_row, strip_rotated, strip_blocks
    ).reshape(column_strip.shape)
    vectors_updated = z_rotated.reshape(vectors_window.shape)
    strip_rows = row_strip.shape[0]
    flat_strip = row_strip.reshape(strip_rows, -1)
    stacked = lax.all_to_all(flat_strip, "row", split_axis=1, concat_axis=0, tiled=True)
    rotated_rows = lax.dot_general(rotation, stacked, (((0,), (0,)), ((), ())), precision=highest)
    returned = lax.all_to_all(rotated_rows, "row", split_axis=0, concat_axis=1, tiled=True)
    column_count = lax.axis_size("col")
    column_rounds = row_strip.shape[1]
    column_block = row_strip.shape[3]
    round_index = jnp.arange(column_rounds, dtype=jnp.int32)[:, None]
    lane_index = jnp.arange(column_block, dtype=jnp.int32)[None, :]
    column_number = (round_index * column_count + column_position) * column_block + lane_index
    row_updated = jnp.where(
        column_number[None, :, None, :] >= start_row + W,
        returned.reshape(row_strip.shape),
        row_strip,
    )
    return (vectors_updated, column_updated, row_updated)


def solution(mesh):
    return jax.shard_map(
        body,
        mesh=mesh,
        in_specs=(
            P(None, "row", None, "col"),
            P(None, "row", None, "col"),
            P("row", None, "col", None),
            P("row", "col"),
            P(),
            P(),
        ),
        out_specs=(
            P(None, "row", None, "col"),
            P(None, "row", None, "col"),
            P("row", None, "col", None),
        ),
        check_vma=False,
    )
```

profile of v0, /device:TPU:1, one launch (start us, length us, event | category | flops | bytes accessed | tf_op | source)
XLA Modules:
  0.0 231.8 jit_solution(5835078651876137352)
XLA Ops:
  7.2 0.7 broadcast_in_dim.44
  7.9 16.6 %all_to_all.106 = f32[8,32,128]{2,1,0:T(8,128)S(1)} all-to-all(f32[8,32,128]{2,1,0:T(8,128)S(1)} %broadcast_in_dim.44), channel_id=1, replica_groups=mesh['row'=32,'col'=8] {'col'}, dimensions={0} | all-to-all | bytes 262144 | tf_op jit(solution)/shard_map/all_to_all | solution.py:11
  24.5 0.7 copy_bitcast_fusion.4
  25.7 4.4 %reduce.3 = f32[32,64,128]{2,1,0:T(8,128)S(1)} reduce(f32[32,64,1,128]{3,2,1,0:T(1,128)} %param.8, f32[]{:T(128)} %broadcast.101), dimensions={2}, to_apply=%param.8.reduce_sub_computation.3 | reduce | bytes 2097156 | tf_op args[2]
  30.5 1.6 copy.61
  32.0 9.4 %all-to-all-start.5 = ((f32[32,32,256]{2,0,1:T(8,128)}), f32[32,32,256]{2,0,1:T(8,128)S(1)}, u32[]{:S(2)}, u32[]{:S(2)}) async-start(f32[32,32,256]{2,0,1:T(8,128)} %copy.61), calls=%async_computation.5 | async-start | bytes 2097152 | tf_op jit(solution)/shard_map/all_to_all | solution.py:76
  41.4 2.8 %copy.74 = f32[32,1,64,128]{3,0,2,1:T(8,128)} copy(f32[32,1,64,128]{3,2,1,0:T(8,128)} %param.6) | data formatting | bytes 2097152 | tf_op args[0]
  44.2 14.1 %all-to-all-done.5 = f32[32,32,256]{2,0,1:T(8,128)S(1)} async-done(((f32[32,32,256]{2,0,1:T(8,128)}), f32[32,32,256]{2,0,1:T(8,128)S(1)}, u32[]{:S(2)}, u32[]{:S(2)}) %all-to-all-start.5) | async-done | bytes 1048608 | tf_op jit(solution)/shard_map/all_to_all | solution.py:76
  58.4 3.6 %all-to-all-start.1 = ((f32[32,64,128]{2,0,1:T(8,128)}), f32[32,64,128]{2,0,1:T(8,128)S(1)}, u32[]{:S(2)}, u32[]{:S(2)}) async-start(f32[32,64,128]{2,0,1:T(8,128)} %bitcast.78), calls=%async_computation.1 | async-start | bytes 2097152 | tf_op jit(solution)/shard_map/all_to_all | solution.py:54
  62.7 1.6 copy.72
  64.2 16.0 %all-gather.2.cloned.1.call-done = f32[1024,1024]{1,0:T(8,128)} async-done(((f32[32,1024]{1,0:T(8,128)}), f32[1024,1024]{1,0:T(8,128)}) %all-gather.2.cloned.1.call-update) | async-done | bytes 4194320 | tf_op jit(solution)/shard_map/all_gather | solution.py:46
  80.3 0.8 slice.8
  81.0 10.2 %all-to-all-done.1 = f32[32,64,128]{2,0,1:T(8,128)S(1)} async-done(((f32[32,64,128]{2,0,1:T(8,128)}), f32[32,64,128]{2,0,1:T(8,128)S(1)}, u32[]{:S(2)}, u32[]{:S(2)}) %all-to-all-start.1) | async-done | bytes 1048608 | tf_op jit(solution)/shard_map/all_to_all | solution.py:54
  91.2 3.7 %all-to-all-start.3 = ((f32[32,64,128]{2,0,1:T(8,128)}), f32[32,64,128]{2,0,1:T(8,128)S(1)}, u32[]{:S(2)}, u32[]{:S(2)}) async-start(f32[32,64,128]{2,0,1:T(8,128)} %bitcast.76), calls=%async_computation.3 | async-start | bytes 2097152 | tf_op jit(solution)/shard_map/all_to_all | solution.py:60
  94.9 0.6 multiply_reduce_fusion
  95.5 1.2 slice.9
  99.4 5.8 %fusion.17 = f32[1,1024]{1,0:T(1,128)S(1)} fusion(f32[1024,1]{0,1:T(1,128)S(1)} %bitcast.101, f32[1024,1024]{1,0:T(8,128)} %all-gather.2.cloned.1.call-done), kind=kOutput, calls=%fused_computation.32 | convolution fusion | flops 12582912 | bytes 4202496 | tf_op jit(solution)/shard_map/dot_general | solution.py:36
  105.3 2.4 %fusion.4 = f32[1024,1024]{0,1:T(8,128)} fusion(f32[1024,1024]{1,0:T(8,128)S(1)} %copy-done, f32[1024]{0:T(1024)S(1)} %bitcast.97, f32[1024]{0:T(1024)S(1)} %broadcast_multiply_fusion), kind=kLoop, calls=%fused_computation.5 | loop fusion | flops 2097152 | bytes 8396800 | tf_op jit(solution)/shard_map/dot_general | solution.py:77
  107.6 5.4 %copy.60 = f32[1024,1024]{1,0:T(8,128)} copy(f32[1024,1024]{0,1:T(8,128)} %fusion.4) | data formatting | bytes 8388608 | tf_op jit(solution)/shard_map/dot_general | solution.py:77
  113.0 6.6 %fusion.18 = f32[32,32,256]{2,1,0:T(8,128)} fusion(f32[32,32,1024]{2,1,0:T(8,128)} %bitcast.85, f32[1024,256,1]{1,0,2:T(8,128)S(1)} %bitcast.92), kind=kOutput, calls=%fused_computation.33 | convolution fusion | flops 3221225472 | bytes 6291456 | tf_op jit(solution)/shard_map/dot_general | solution.py:77
  119.6 2.3 %all-to-all-done.3 = f32[32,64,128]{2,0,1:T(8,128)S(1)} async-done(((f32[32,64,128]{2,0,1:T(8,128)}), f32[32,64,128]{2,0,1:T(8,128)S(1)}, u32[]{:S(2)}, u32[]{:S(2)}) %all-to-all-start.3) | async-done | bytes 1048608 | tf_op jit(solution)/shard_map/all_to_all | solution.py:60
  121.9 5.0 %all-to-all-start.6 = ((f32[32,32,256]{2,1,0:T(8,128)}), f32[32,32,256]{2,1,0:T(8,128)S(1)}, u32[]{:S(2)}, u32[]{:S(2)}) async-start(f32[32,32,256]{2,1,0:T(8,128)} %fusion.18), calls=%async_computation.6 | async-start | bytes 2097152 | tf_op jit(solution)/shard_map/all_to_all | solution.py:78
  126.9 1.6 copy.73
  128.5 2.4 %all_to_all.81 = f32[32,8,1024]{2,0,1:T(8,128)} reshape(f32[32,8,8,128]{3,2,0,1:T(8,128)} %bitcast.90) | data formatting | bytes 2097152 | tf_op jit(solution)/shard_map/all_to_all | solution.py:54
  130.8 6.4 %fusion.9 = f32[32,8,1024]{2,0,1:T(8,128)S(1)} fusion(f32[32,8,1024]{2,0,1:T(8,128)} %all_to_all.81, f32[1024,1024]{1,0:T(8,128)} %all-gather.2.cloned.1.call-done, f32[1024]{0:T(1024)S(1)} %bitcast.98, f32[1024]{0:T(1024)S(1)} %broadcast_multiply_fusion), kind=kOutput, calls=%fused_computation.10 | convolution fusion | flops 3223322624 | bytes 6299648 | tf_op jit(solution)/shard_map/rbk,kj->rbj/dot_general | solution.py:52
  137.2 2.7 %copy.54 = f32[32,8,1024]{0,1,2:T(8,128)} copy(f32[32,8,1024]{2,0,1:T(8,128)S(1)} %fusion.9) | data formatting | bytes 2097152 | tf_op jit(solution)/shard_map/rbk,kj->rbj/dot_general | solution.py:52
  140.0 4.8 %reshape.143 = f32[8,1,32768]{2,1,0:T(1,128)} reshape(f32[1024,8,32]{2,1,0:T(8,128)} %bitcast.81) | data formatting | bytes 2097152
  144.8 1.0 copy-done.4
  145.8 4.3 %all-to-all-start.2 = ((f32[8,1,32768]{2,1,0:T(1,128)}), f32[8,1,32768]{2,1,0:T(1,128)S(1)}, u32[]{:S(2)}, u32[]{:S(2)}) async-start(f32[8,1,32768]{2,1,0:T(1,128)} %reshape.143), calls=%async_computation.2 | async-start | bytes 2097152 | tf_op jit(solution)/shard_map/all_to_all | solution.py:64
  150.1 0.6 copy.71
  150.7 1.1 all_to_all.88
  151.8 6.4 %fusion.12 = f32[32,8,1024]{2,0,1:T(8,128)S(1)} fusion(f32[32,8,1024]{2,0,1:T(8,128)} %all_to_all.88, f32[1024,1024]{1,0:T(8,128)} %all-gather.2.cloned.1.call-done, f32[1024]{0:T(1024)S(1)} %bitcast.99, f32[1024]{0:T(1024)S(1)} %broadcast_multiply_fusion), kind=kOutput, calls=%fused_computation.11 | convolution fusion | flops 3223322624 | bytes 6299648 | tf_op jit(solution)/shard_map/rbk,kj->rbj/dot_general | solution.py:58
  158.2 2.7 %copy.58 = f32[32,8,1024]{0,1,2:T(8,128)} copy(f32[32,8,1024]{2,0,1:T(8,128)S(1)} %fusion.12) | data formatting | bytes 2097152 | tf_op jit(solution)/shard_map/rbk,kj->rbj/dot_general | solution.py:58
  160.9 4.9 %reshape.145 = f32[8,1,32768]{2,1,0:T(1,128)} reshape(f32[1024,8,32]{2,1,0:T(8,128)} %bitcast.82) | data formatting | bytes 2097152
  165.9 13.5 %all-to-all-done.2 = f32[8,1,32768]{2,1,0:T(1,128)S(1)} async-done(((f32[8,1,32768]{2,1,0:T(1,128)}), f32[8,1,32768]{2,1,0:T(1,128)S(1)}, u32[]{:S(2)}, u32[]{:S(2)}) %all-to-all-start.2) | async-done | bytes 1048608 | tf_op jit(solution)/shard_map/all_to_all | solution.py:64
  179.3 4.2 %all-to-all-start.4 = ((f32[8,1,32768]{2,1,0:T(1,128)}), f32[8,1,32768]{2,1,0:T(1,128)}, u32[]{:S(2)}, u32[]{:S(2)}) async-start(f32[8,1,32768]{2,1,0:T(1,128)} %reshape.145), calls=%async_computation.4 | async-start | bytes 2097152 | tf_op jit(solution)/shard_map/all_to_all | solution.py:65
  184.4 1.6 copy.62
  186.0 1.3 reshape.129
  187.3 1.1 broadcast_select_fusion
  188.4 0.5 broadcast.102
  189.0 3.1 %reduce.4 = f32[8,32768]{1,0:T(8,128)S(1)} reduce(f32[8,1,32768]{2,1,0:T(1,128)S(1)} %all-to-all-done.2, f32[]{:T(128)} %broadcast.102), dimensions={1}, to_apply=%all_to_all.82.reduce_sub_computation | reduce | bytes 2097156 | tf_op jit(solution)/shard_map/all_to_all | solution.py:64
  192.0 3.3 %reshape.144 = f32[1024,8,32]{2,1,0:T(8,128)} reshape(f32[8,32768]{1,0:T(8,128)S(1)} %reduce.4) | data formatting | bytes 2097152
  195.3 3.9 %copy.55 = f32[32,8,8,128]{3,2,1,0:T(8,128)} copy(f32[32,8,8,128]{0,2,3,1:T(8,128)} %bitcast.83) | data formatting | bytes 2097152 | tf_op jit(solution)/shard_map/all_to_all | solution.py:64
  199.3 13.5 %all-to-all-done.4 = f32[8,1,32768]{2,1,0:T(1,128)} async-done(((f32[8,1,32768]{2,1,0:T(1,128)}), f32[8,1,32768]{2,1,0:T(1,128)}, u32[]{:S(2)}, u32[]{:S(2)}) %all-to-all-start.4) | async-done | bytes 1048608 | tf_op jit(solution)/shard_map/all_to_all | solution.py:65
  212.8 4.3 %reduce.5 = f32[8,32768]{1,0:T(8,128)S(1)} reduce(f32[8,1,32768]{2,1,0:T(1,128)} %all-to-all-done.4, f32[]{:T(128)} %broadcast.102), dimensions={1}, to_apply=%all_to_all.89.reduce_sub_computation | reduce | bytes 2097156 | tf_op jit(solution)/shard_map/all_to_all | solution.py:65
  217.1 3.3 %reshape.146 = f32[1024,8,32]{2,1,0:T(8,128)} reshape(f32[8,32768]{1,0:T(8,128)S(1)} %reduce.5) | data formatting | bytes 2097152
  220.4 3.2 %copy.59 = f32[32,8,8,128]{3,2,1,0:T(8,128)S(1)} copy(f32[32,8,8,128]{0,2,3,1:T(8,128)} %bitcast.84) | data formatting | bytes 2097152 | tf_op jit(solution)/shard_map/all_to_all | solution.py:65
  223.7 1.3 bitcast_select_fusion
  (23 shorter events, 1.1 us)
Async XLA Ops:
  7.2 73.1 %all-gather.2.cloned.1.call-start = ((), (), s32[]{:S(2)}) async-start(), calls=%async_computation.7 | async-start | bytes 4325376 | tf_op jit(solution)/shard_map/all_gather | solution.py:46
  30.5 32.2 %copy-start.2 = (f32[32,1,64,128]{3,2,1,0:T(8,128)S(1)}, f32[32,1,64,128]{3,2,1,0:T(8,128)}, u32[]{:S(2)}) copy-start(f32[32,1,64,128]{3,2,1,0:T(8,128)} %param.7) | copy-start | bytes 3145732
  32.0 26.3 %all-to-all-start.5 = ((f32[32,32,256]{2,0,1:T(8,128)}), f32[32,32,256]{2,0,1:T(8,128)S(1)}, u32[]{:S(2)}, u32[]{:S(2)}) async-start(f32[32,32,256]{2,0,1:T(8,128)} %copy.61), calls=%async_computation.5 | async-start | bytes 2097152 | tf_op jit(solution)/shard_map/all_to_all | solution.py:76
  58.4 32.8 %all-to-all-start.1 = ((f32[32,64,128]{2,0,1:T(8,128)}), f32[32,64,128]{2,0,1:T(8,128)S(1)}, u32[]{:S(2)}, u32[]{:S(2)}) async-start(f32[32,64,128]{2,0,1:T(8,128)} %bitcast.78), calls=%async_computation.1 | async-start | bytes 2097152 | tf_op jit(solution)/shard_map/all_to_all | solution.py:54
  91.2 30.7 %all-to-all-start.3 = ((f32[32,64,128]{2,0,1:T(8,128)}), f32[32,64,128]{2,0,1:T(8,128)S(1)}, u32[]{:S(2)}, u32[]{:S(2)}) async-start(f32[32,64,128]{2,0,1:T(8,128)} %bitcast.76), calls=%async_computation.3 | async-start | bytes 2097152 | tf_op jit(solution)/shard_map/all_to_all | solution.py:60
  99.4 5.8 %copy-start = (f32[1024,1024]{1,0:T(8,128)S(1)}, f32[1024,1024]{1,0:T(8,128)}, u32[]{:S(2)}) copy-start(f32[1024,1024]{1,0:T(8,128)} %all-gather.2.cloned.1.call-done) | copy-start | bytes 12582916
  121.9 22.9 %all-to-all-start.6 = ((f32[32,32,256]{2,1,0:T(8,128)}), f32[32,32,256]{2,1,0:T(8,128)S(1)}, u32[]{:S(2)}, u32[]{:S(2)}) async-start(f32[32,32,256]{2,1,0:T(8,128)} %fusion.18), calls=%async_computation.6 | async-start | bytes 2097152 | tf_op jit(solution)/shard_map/all_to_all | solution.py:78
  144.8 1.0 copy-start.4
  145.8 33.6 %all-to-all-start.2 = ((f32[8,1,32768]{2,1,0:T(1,128)}), f32[8,1,32768]{2,1,0:T(1,128)S(1)}, u32[]{:S(2)}, u32[]{:S(2)}) async-start(f32[8,1,32768]{2,1,0:T(1,128)} %reshape.143), calls=%async_computation.2 | async-start | bytes 2097152 | tf_op jit(solution)/shard_map/all_to_all | solution.py:64
  160.9 23.5 %copy-start.5 = (f32[32,32,256]{2,1,0:T(8,128)S(1)}, f32[32,32,256]{2,1,0:T(8,128)}, u32[]{:S(2)}) copy-start(f32[32,32,256]{2,1,0:T(8,128)} %copy-done.4) | copy-start | bytes 3145732
  165.9 21.5 %copy-start.1 = (f32[32,64,1,128]{3,2,1,0:T(1,128)S(1)}, f32[32,64,1,128]{3,2,1,0:T(1,128)}, u32[]{:S(2)}) copy-start(f32[32,64,1,128]{3,2,1,0:T(1,128)} %param.8) | copy-start | bytes 3145732
  179.3 33.5 %all-to-all-start.4 = ((f32[8,1,32768]{2,1,0:T(1,128)}), f32[8,1,32768]{2,1,0:T(1,128)}, u32[]{:S(2)}, u32[]{:S(2)}) async-start(f32[8,1,32768]{2,1,0:T(1,128)} %reshape.145), calls=%async_computation.4 | async-start | bytes 2097152 | tf_op jit(solution)/shard_map/all_to_all | solution.py:65
  217.1 6.5 %copy-start.3 = (f32[32,1,64,128]{3,2,1,0:T(8,128)S(1)}, f32[32,1,64,128]{3,2,1,0:T(8,128)}, u32[]{:S(2)}) copy-start(f32[32,1,64,128]{3,2,1,0:T(8,128)} %param.7) | copy-start | bytes 3145732
Sparse Core Ops, SparseCore 0:
  25.3 54.9 all-gather.1
where the time goes:
time: 233 us; the launch traced here: 232 us
  waiting for transfers between devices  69.7 us (30%)
  local copies, waits for them, and re-layouts  54.5 us (23%)
  starting transfers between devices  30.3 us (13%)
  matrix products  25.2 us (11%)
  between operations  18.2 us (8%)
  other arithmetic  17.4 us (7%)
  blocking collectives  16.6 us (7%)
    unnamed x19, local copies, waits for them, and re-layouts  22.3 us
    all_to_all x1, blocking collectives, from_everyone(): lax.all_to_all(jnp.broadcast_to(x[None], (peers, *x.shape)), axis, 0, 0,...  16.6 us
    all_gather x1, waiting for transfers between devices, body(): lax.all_gather(widened, 'row', axis=0, tiled=True)  16 us
    all_to_all x1, waiting for transfers between devices, body(): lax.all_to_all(flat_strip, 'row', split_axis=1, concat_axis=0, tiled=True)  14.1 us
    all_to_all x1, waiting for transfers between devices, body(): lax.all_to_all(strip_turned, 'col', split_axis=2, concat_axis=1, tiled=True)  13.5 us
    all_to_all x1, waiting for transfers between devices, body(): lax.all_to_all(z_turned, 'col', split_axis=2, concat_axis=1, tiled=True)  13.5 us
    all_to_all x1, waiting for transfers between devices, body(): lax.all_to_all(z_blocks, 'col', split_axis=1, concat_axis=2, tiled=True)  10.2 us
    all_to_all x1, starting transfers between devices, body(): lax.all_to_all(flat_strip, 'row', split_axis=1, concat_axis=0, tiled=True)  9.38 us
  transfers between devices with their start and end apart: 7, of which 6 were waited for; matrix products, arithmetic and copies ran while one was open for 34% of the time, Pallas kernels for 0%

commit v1 on v0

--- a/solution.py
+++ b/solution.py
@@ -43,7 +43,12 @@
     column_position = lax.axis_index("col")
     start_row = window_start[0]
     widened = gather_directly(factor, "col", 1)
-    rotation = reflect(lax.all_gather(widened, "row", axis=0, tiled=True), deflated)
+    rotation = reflect(
+        jnp.concatenate(
+            lax.all_to_all(jnp.stack([widened] * lax.axis_size("row")), "row", 0, 0), axis=0
+        ),
+        deflated,
+    )
     rounds = vectors_window.shape[0]
     blocks = vectors_window.shape[2]
     local_width = vectors_window.shape[3]

time: 233 us -> 279 us (1.20)
  waiting for transfers between devices: 69.7 us -> 119 us
  starting transfers between devices: 30.3 us -> 50.3 us
  blocking collectives: 16.6 us -> 0 us
  between operations: 18.2 us -> 4.68 us
  other arithmetic: 17.4 us -> 23.2 us
  local copies, waits for them, and re-layouts: 54.5 us -> 59 us
  matrix products: 25.2 us -> 22 us
    all_to_all x0 -> x2, waiting for transfers between devices: none -> 50 us  [the longest x1 49.1 us: body(): lax.all_to_all(jnp.stack([widened] * lax.axis_size('row')), 'row', 0, 0)]
    all_to_all x1, waiting for transfers between devices: 10.2 us -> 29.2 us  [body(): lax.all_to_all(z_blocks, 'col', split_axis=1, concat_axis=2, tiled=True)]
    all_to_all x1 -> x0, blocking collectives: 16.6 us -> none  [from_everyone(): lax.all_to_all(jnp.broadcast_to(x[None], (peers, *x.shape)), axis, 0, 0,...]
    all_gather x1 -> x0, waiting for transfers between devices: 16 us -> none  [body(): lax.all_gather(widened, 'row', axis=0, tiled=True)]
    all_to_all x0 -> x2, starting transfers between devices: none -> 14.1 us  [the longest x1 9 us: from_everyone(): lax.all_to_all(jnp.broadcast_to(x[None], (peers, *x.shape)), axis, 0, 0,...]
    unnamed x19 -> x21, local copies, waits for them, and re-layouts: 22.3 us -> 24.3 us
  transfers between devices with their start and end apart: 7 -> 8, of which waited for: 6 -> 6; matrix products, arithmetic and copies ran while one was open for 34% -> 29% of each run, Pallas kernels for 0% -> 0%
where the time goes in v1:
time: 279 us; the launch traced here: 278 us
  waiting for transfers between devices  119 us (43%)
  local copies, waits for them, and re-layouts  59 us (21%)
  starting transfers between devices  50.3 us (18%)
  other arithmetic  23.2 us (8%)
  matrix products  22 us (8%)
  between operations  4.68 us (2%)
    all_to_all x1, waiting for transfers between devices, body(): lax.all_to_all(jnp.stack([widened] * lax.axis_size('row')), 'row', 0, 0)  49.1 us
    all_to_all x1, waiting for transfers between devices, body(): lax.all_to_all(z_blocks, 'col', split_axis=1, concat_axis=2, tiled=True)  29.2 us
    unnamed x21, local copies, waits for them, and re-layouts  24.3 us
    all_to_all x1, waiting for transfers between devices, body(): lax.all_to_all(flat_strip, 'row', split_axis=1, concat_axis=0, tiled=True)  14.2 us
    all_to_all x1, waiting for transfers between devices, body(): lax.all_to_all(z_turned, 'col', split_axis=2, concat_axis=1, tiled=True)  13.9 us
    all_to_all x1, waiting for transfers between devices, body(): lax.all_to_all(strip_turned, 'col', split_axis=2, concat_axis=1, tiled=True)  11.4 us
    all_to_all x1, starting transfers between devices, body(): lax.all_to_all(flat_strip, 'row', split_axis=1, concat_axis=0, tiled=True)  9.38 us
    all_to_all x1, starting transfers between devices, from_everyone(): lax.all_to_all(jnp.broadcast_to(x[None], (peers, *x.shape)), axis, 0, 0,...  9 us
  transfers between devices with their start and end apart: 8, of which 6 were waited for; matrix products, arithmetic and copies ran while one was open for 29% of the time, Pallas kernels for 0%

profile of v1, /device:TPU:1, one launch (start us, length us, event | category | flops | bytes accessed | tf_op | source)
XLA Modules:
  0.0 277.9 jit_solution(11860968942480630681)
XLA Ops:
  0.6 1.4 broadcast_in_dim.42
  2.0 9.0 %all-to-all-start = ((f32[8,32,128]{2,1,0:T(8,128)}), f32[8,32,128]{2,1,0:T(8,128)S(1)}, u32[]{:S(2)}, u32[]{:S(2)}) async-start(f32[8,32,128]{2,1,0:T(8,128)} %broadcast_in_dim.42), calls=%async_computation | async-start | bytes 262144 | tf_op jit(solution)/shard_map/all_to_all | solution.py:11
  11.5 4.4 %reduce.3 = f32[32,64,128]{2,1,0:T(8,128)S(1)} reduce(f32[32,64,1,128]{3,2,1,0:T(1,128)} %param.8, f32[]{:T(128)} %broadcast.118), dimensions={2}, to_apply=%param.8.reduce_sub_computation.3 | reduce | bytes 2097156 | tf_op args[2]
  16.3 1.6 copy.56
  17.9 0.9 all-to-all-done
  18.8 9.4 %all-to-all-start.6 = ((f32[32,32,256]{2,0,1:T(8,128)}), f32[32,32,256]{2,0,1:T(8,128)S(1)}, u32[]{:S(2)}, u32[]{:S(2)}) async-start(f32[32,32,256]{2,0,1:T(8,128)} %copy.56), calls=%async_computation.6 | async-start | bytes 2097152 | tf_op jit(solution)/shard_map/all_to_all | solution.py:81
  28.2 2.8 %copy.69 = f32[32,1,64,128]{3,0,2,1:T(8,128)} copy(f32[32,1,64,128]{3,2,1,0:T(8,128)} %param.6) | data formatting | bytes 2097152 | tf_op args[0]
  31.0 14.2 %all-to-all-done.6 = f32[32,32,256]{2,0,1:T(8,128)S(1)} async-done(((f32[32,32,256]{2,0,1:T(8,128)}), f32[32,32,256]{2,0,1:T(8,128)S(1)}, u32[]{:S(2)}, u32[]{:S(2)}) %all-to-all-start.6) | async-done | bytes 1048608 | tf_op jit(solution)/shard_map/all_to_all | solution.py:81
  45.2 4.7 %all-to-all-start.2 = ((f32[32,64,128]{2,0,1:T(8,128)}), f32[32,64,128]{2,0,1:T(8,128)S(1)}, u32[]{:S(2)}, u32[]{:S(2)}) async-start(f32[32,64,128]{2,0,1:T(8,128)} %bitcast.77), calls=%async_computation.2 | async-start | bytes 2097152 | tf_op jit(solution)/shard_map/all_to_all | solution.py:59
  49.9 29.2 %all-to-all-done.2 = f32[32,64,128]{2,0,1:T(8,128)S(1)} async-done(((f32[32,64,128]{2,0,1:T(8,128)}), f32[32,64,128]{2,0,1:T(8,128)S(1)}, u32[]{:S(2)}, u32[]{:S(2)}) %all-to-all-start.2) | async-done | bytes 1048608 | tf_op jit(solution)/shard_map/all_to_all | solution.py:59
  79.1 2.5 stack.3
  81.6 5.0 %all-to-all-start.1 = ((f32[32,32,1024]{2,1,0:T(8,128)}), f32[32,32,1024]{2,1,0:T(8,128)}, u32[]{:S(2)}, u32[]{:S(2)}) async-start(f32[32,32,1024]{2,1,0:T(8,128)} %stack.3), calls=%async_computation.1 | async-start | bytes 8388608 | tf_op jit(solution)/shard_map/all_to_all | solution.py:48
  86.7 1.6 copy.67
  88.3 49.1 %all-to-all-done.1 = f32[32,32,1024]{2,1,0:T(8,128)} async-done(((f32[32,32,1024]{2,1,0:T(8,128)}), f32[32,32,1024]{2,1,0:T(8,128)}, u32[]{:S(2)}, u32[]{:S(2)}) %all-to-all-start.1) | async-done | bytes 4194336 | tf_op jit(solution)/shard_map/all_to_all | solution.py:48
  137.4 3.7 %all-to-all-start.4 = ((f32[32,64,128]{2,0,1:T(8,128)}), f32[32,64,128]{2,0,1:T(8,128)S(1)}, u32[]{:S(2)}, u32[]{:S(2)}) async-start(f32[32,64,128]{2,0,1:T(8,128)} %bitcast.75), calls=%async_computation.4 | async-start | bytes 2097152 | tf_op jit(solution)/shard_map/all_to_all | solution.py:65
  141.8 1.2 slice.9
  146.9 0.8 fusion
  147.6 5.6 %fusion.1 = f32[1,1024]{1,0:T(1,128)S(1)} fusion(f32[1024,1024]{1,0:T(8,128)} %bitcast.2, f32[1,1024]{1,0:T(1,128)S(1)} %fusion), kind=kOutput, calls=%fused_computation.16 | convolution fusion | flops 12582912 | bytes 4202496 | tf_op jit(solution)/shard_map/dot_general | solution.py:36
  153.3 4.6 %subtract_bitcast_fusion = f32[1024,1024]{0,1:T(8,128)} fusion(f32[1024]{0:T(1024)S(1)} %bitcast.96, f32[1024]{0:T(1024)S(1)} %broadcast_multiply_fusion, f32[32,32,1024]{2,1,0:T(8,128)} %all-to-all-done.1), kind=kLoop, calls=%fused_computation | loop fusion | flops 2097152 | bytes 8396800 | tf_op jit(solution)/shard_map/dot_general | solution.py:82
  157.9 5.4 %copy.55 = f32[1024,1024]{1,0:T(8,128)} copy(f32[1024,1024]{0,1:T(8,128)} %subtract_bitcast_fusion) | data formatting | bytes 8388608 | tf_op jit(solution)/shard_map/dot_general | solution.py:82
  163.2 6.6 %fusion.3 = f32[32,32,256]{2,1,0:T(8,128)} fusion(f32[32,32,1024]{2,1,0:T(8,128)} %bitcast.84, f32[1024,256,1]{1,0,2:T(8,128)S(1)} %bitcast.93), kind=kOutput, calls=%fused_computation.23 | convolution fusion | flops 3221225472 | bytes 6291456 | tf_op jit(solution)/shard_map/dot_general | solution.py:82
  169.8 7.3 %all-to-all-start.7 = ((f32[32,32,256]{2,1,0:T(8,128)}), f32[32,32,256]{2,1,0:T(8,128)S(1)}, u32[]{:S(2)}, u32[]{:S(2)}) async-start(f32[32,32,256]{2,1,0:T(8,128)} %fusion.3), calls=%async_computation.7 | async-start | bytes 2097152 | tf_op jit(solution)/shard_map/all_to_all | solution.py:83
  177.1 1.6 copy.68
  178.7 2.4 all_to_all.85
  181.1 2.7 multiply_subtract_fusion
  183.8 1.9 copy-done.5
  185.7 3.8 %convolution_bitcast_fusion.1 = f32[32,8,1024]{2,0,1:T(8,128)S(1)} fusion(f32[1024,1024,1]{1,0,2:T(8,128)S(1)} %bitcast.91, f32[32,8,1024]{2,0,1:T(8,128)S(1)} %copy-done.6), kind=kOutput, calls=%fused_computation.3 | convolution fusion | flops 3221225472 | bytes 6291456 | tf_op jit(solution)/shard_map/rbk,kj->rbj/dot_general | solution.py:57
  189.6 2.7 copy.49
  192.3 4.8 %reshape.168 = f32[8,1,32768]{2,1,0:T(1,128)} reshape(f32[1024,8,32]{2,1,0:T(8,128)} %bitcast.80) | data formatting | bytes 2097152
  197.1 1.0 copy-done.3
  198.1 6.7 %all-to-all-start.3 = ((f32[8,1,32768]{2,1,0:T(1,128)}), f32[8,1,32768]{2,1,0:T(1,128)S(1)}, u32[]{:S(2)}, u32[]{:S(2)}) async-start(f32[8,1,32768]{2,1,0:T(1,128)} %reshape.168), calls=%async_computation.3 | async-start | bytes 2097152 | tf_op jit(solution)/shard_map/all_to_all | solution.py:69
  205.4 1.1 all_to_all.92
  206.5 6.0 %convolution_bitcast_fusion = f32[32,8,1024]{2,0,1:T(8,128)S(1)} fusion(f32[1024,1024,1]{1,0,2:T(8,128)} %bitcast.92, f32[32,8,1024]{2,0,1:T(8,128)} %all_to_all.92), kind=kOutput, calls=%fused_computation.2 | convolution fusion | flops 3221225472 | bytes 6291456 | tf_op jit(solution)/shard_map/rbk,kj->rbj/dot_general | solution.py:63
  212.5 2.7 copy.53
  215.2 4.9 %reshape.170 = f32[8,1,32768]{2,1,0:T(1,128)} reshape(f32[1024,8,32]{2,1,0:T(8,128)} %bitcast.81) | data formatting | bytes 2097152
  220.1 13.9 %all-to-all-done.3 = f32[8,1,32768]{2,1,0:T(1,128)S(1)} async-done(((f32[8,1,32768]{2,1,0:T(1,128)}), f32[8,1,32768]{2,1,0:T(1,128)S(1)}, u32[]{:S(2)}, u32[]{:S(2)}) %all-to-all-start.3) | async-done | bytes 1048608 | tf_op jit(solution)/shard_map/all_to_all | solution.py:69
  234.0 4.5 %all-to-all-start.5 = ((f32[8,1,32768]{2,1,0:T(1,128)}), f32[8,1,32768]{2,1,0:T(1,128)}, u32[]{:S(2)}, u32[]{:S(2)}) async-start(f32[8,1,32768]{2,1,0:T(1,128)} %reshape.170), calls=%async_computation.5 | async-start | bytes 2097152 | tf_op jit(solution)/shard_map/all_to_all | solution.py:70
  239.4 1.6 copy.57
  241.0 1.3 reshape.154
  242.3 1.1 broadcast_select_fusion
  244.0 3.1 %reduce.4 = f32[8,32768]{1,0:T(8,128)S(1)} reduce(f32[8,1,32768]{2,1,0:T(1,128)S(1)} %all-to-all-done.3, f32[]{:T(128)} %broadcast.119), dimensions={1}, to_apply=%all_to_all.86.reduce_sub_computation | reduce | bytes 2097156 | tf_op jit(solution)/shard_map/all_to_all | solution.py:69
  247.1 3.3 %reshape.169 = f32[1024,8,32]{2,1,0:T(8,128)} reshape(f32[8,32768]{1,0:T(8,128)S(1)} %reduce.4) | data formatting | bytes 2097152
  250.4 3.9 %copy.50 = f32[32,8,8,128]{3,2,1,0:T(8,128)} copy(f32[32,8,8,128]{0,2,3,1:T(8,128)} %bitcast.82) | data formatting | bytes 2097152 | tf_op jit(solution)/shard_map/all_to_all | solution.py:69
  254.3 11.4 %all-to-all-done.5 = f32[8,1,32768]{2,1,0:T(1,128)} async-done(((f32[8,1,32768]{2,1,0:T(1,128)}), f32[8,1,32768]{2,1,0:T(1,128)}, u32[]{:S(2)}, u32[]{:S(2)}) %all-to-all-start.5) | async-done | bytes 1048608 | tf_op jit(solution)/shard_map/all_to_all | solution.py:70
  265.7 4.4 %reduce.5 = f32[8,32768]{1,0:T(8,128)S(1)} reduce(f32[8,1,32768]{2,1,0:T(1,128)} %all-to-all-done.5, f32[]{:T(128)} %broadcast.119), dimensions={1}, to_apply=%all_to_all.93.reduce_sub_computation | reduce | bytes 2097156 | tf_op jit(solution)/shard_map/all_to_all | solution.py:70
  270.1 3.3 %reshape.171 = f32[1024,8,32]{2,1,0:T(8,128)} reshape(f32[8,32768]{1,0:T(8,128)S(1)} %reduce.5) | data formatting | bytes 2097152
  273.4 3.2 %copy.54 = f32[32,8,8,128]{3,2,1,0:T(8,128)S(1)} copy(f32[32,8,8,128]{0,2,3,1:T(8,128)} %bitcast.83) | data formatting | bytes 2097152 | tf_op jit(solution)/shard_map/all_to_all | solution.py:70
  276.6 1.3 bitcast_select_fusion
  (27 shorter events, 3.6 us)
Async XLA Ops:
  2.0 16.8 %all-to-all-start = ((f32[8,32,128]{2,1,0:T(8,128)}), f32[8,32,128]{2,1,0:T(8,128)S(1)}, u32[]{:S(2)}, u32[]{:S(2)}) async-start(f32[8,32,128]{2,1,0:T(8,128)} %broadcast_in_dim.42), calls=%async_computation | async-start | bytes 262144 | tf_op jit(solution)/shard_map/all_to_all | solution.py:11
  18.8 26.4 %all-to-all-start.6 = ((f32[32,32,256]{2,0,1:T(8,128)}), f32[32,32,256]{2,0,1:T(8,128)S(1)}, u32[]{:S(2)}, u32[]{:S(2)}) async-start(f32[32,32,256]{2,0,1:T(8,128)} %copy.56), calls=%async_computation.6 | async-start | bytes 2097152 | tf_op jit(solution)/shard_map/all_to_all | solution.py:81
  45.2 33.9 %all-to-all-start.2 = ((f32[32,64,128]{2,0,1:T(8,128)}), f32[32,64,128]{2,0,1:T(8,128)S(1)}, u32[]{:S(2)}, u32[]{:S(2)}) async-start(f32[32,64,128]{2,0,1:T(8,128)} %bitcast.77), calls=%async_computation.2 | async-start | bytes 2097152 | tf_op jit(solution)/shard_map/all_to_all | solution.py:59
  81.6 5.1 %copy-start.1 = (f32[32,1,64,128]{3,2,1,0:T(8,128)S(1)}, f32[32,1,64,128]{3,2,1,0:T(8,128)}, u32[]{:S(2)}) copy-start(f32[32,1,64,128]{3,2,1,0:T(8,128)} %param.7) | copy-start | bytes 3145732
  81.6 55.8 %all-to-all-start.1 = ((f32[32,32,1024]{2,1,0:T(8,128)}), f32[32,32,1024]{2,1,0:T(8,128)}, u32[]{:S(2)}, u32[]{:S(2)}) async-start(f32[32,32,1024]{2,1,0:T(8,128)} %stack.3), calls=%async_computation.1 | async-start | bytes 8388608 | tf_op jit(solution)/shard_map/all_to_all | solution.py:48
  137.4 32.4 %all-to-all-start.4 = ((f32[32,64,128]{2,0,1:T(8,128)}), f32[32,64,128]{2,0,1:T(8,128)S(1)}, u32[]{:S(2)}, u32[]{:S(2)}) async-start(f32[32,64,128]{2,0,1:T(8,128)} %bitcast.75), calls=%async_computation.4 | async-start | bytes 2097152 | tf_op jit(solution)/shard_map/all_to_all | solution.py:65
  169.8 27.3 %all-to-all-start.7 = ((f32[32,32,256]{2,1,0:T(8,128)}), f32[32,32,256]{2,1,0:T(8,128)S(1)}, u32[]{:S(2)}, u32[]{:S(2)}) async-start(f32[32,32,256]{2,1,0:T(8,128)} %fusion.3), calls=%async_computation.7 | async-start | bytes 2097152 | tf_op jit(solution)/shard_map/all_to_all | solution.py:83
  181.1 4.6 %copy-start.6 = (f32[32,8,1024]{2,0,1:T(8,128)S(1)}, f32[32,8,1024]{2,0,1:T(8,128)}, u32[]{:S(2)}) copy-start(f32[32,8,1024]{2,0,1:T(8,128)} %all_to_all.85) | copy-start | bytes 3145732
  183.8 2.0 copy-start.5
  197.1 1.0 copy-start.3
  198.1 35.9 %all-to-all-start.3 = ((f32[8,1,32768]{2,1,0:T(1,128)}), f32[8,1,32768]{2,1,0:T(1,128)S(1)}, u32[]{:S(2)}, u32[]{:S(2)}) async-start(f32[8,1,32768]{2,1,0:T(1,128)} %reshape.168), calls=%async_computation.3 | async-start | bytes 2097152 | tf_op jit(solution)/shard_map/all_to_all | solution.py:69
  215.2 24.1 %copy-start.4 = (f32[32,32,256]{2,1,0:T(8,128)S(1)}, f32[32,32,256]{2,1,0:T(8,128)}, u32[]{:S(2)}) copy-start(f32[32,32,256]{2,1,0:T(8,128)} %copy-done.3) | copy-start | bytes 3145732
  220.1 22.1 %copy-start = (f32[32,64,1,128]{3,2,1,0:T(1,128)S(1)}, f32[32,64,1,128]{3,2,1,0:T(1,128)}, u32[]{:S(2)}) copy-start(f32[32,64,1,128]{3,2,1,0:T(1,128)} %param.8) | copy-start | bytes 3145732
  234.0 31.7 %all-to-all-start.5 = ((f32[8,1,32768]{2,1,0:T(1,128)}), f32[8,1,32768]{2,1,0:T(1,128)}, u32[]{:S(2)}, u32[]{:S(2)}) async-start(f32[8,1,32768]{2,1,0:T(1,128)} %reshape.170), calls=%async_computation.5 | async-start | bytes 2097152 | tf_op jit(solution)/shard_map/all_to_all | solution.py:70
  270.1 6.6 %copy-start.2 = (f32[32,1,64,128]{3,2,1,0:T(8,128)S(1)}, f32[32,1,64,128]{3,2,1,0:T(8,128)}, u32[]{:S(2)}) copy-start(f32[32,1,64,128]{3,2,1,0:T(8,128)} %param.7) | copy-start | bytes 3145732
